TPU v7x, 256 devices: a whole 4x4x8 slice. The times are simulated.
256 devices in a mesh: first: 16 (over y, x), second: 16 (over z, core).
Axes of the slice: x: 4, y: 4, z: 8, core: 2. Of those that a mesh axis runs over, the one named last changes fastest.
Arguments:
- pair_state: bfloat16 [768, 768, 128], P('first', 'second'), may hold values from -6 to 6
- in_gain: float32 [128], replicated, may hold values from 0.25 to 1.75
- left_weight: bfloat16 [128, 128], replicated, may hold values from -0.5 to 0.5
- right_weight: bfloat16 [128, 128], replicated, may hold values from -0.5 to 0.5
- mid_gain: float32 [128], replicated, may hold values from 0.25 to 1.75
- out_weight: bfloat16 [128, 128], replicated, may hold values from -0.5 to 0.5
- out_gate: bfloat16 [128, 128], replicated, may hold values from -0.5 to 0.5
Outputs:
- triangle_out: bfloat16 [768, 768, 128], P('first', 'second')
All inputs are finite; a program needn't handle non-finite values.
Results may differ from a plain program's by a relative error of at most 0.015.
Values may be sent and summed in bfloat16 or wider, within the bound.
A program may use at most 64 MiB of HBM per device.

v0:
```python
import jax
import jax.numpy as jnp
from jax import lax
from jax.sharding import PartitionSpec as P


def unit_channels(values, channel_gain):
    centred = values - jnp.mean(values, axis=-1, keepdims=True)
    return (
        centred
        * lax.rsqrt(jnp.mean(centred * centred, axis=-1, keepdims=True) + 1e-05)
        * channel_gain
    )


def make_factors(pair_in, in_gain, left_weight, right_weight):
    ready = unit_channels(pair_in.astype(jnp.float32), in_gain).astype(jnp.bfloat16)
    ready = lax.optimization_barrier(ready)
    left = jnp.einsum("ijc,cd->ijd", ready, left_weight, preferred_element_type=jnp.float32)
    right = jnp.einsum("ijc,cd->ijd", ready, right_weight, preferred_element_type=jnp.float32)
    return (ready, left.astype(jnp.bfloat16), right.astype(jnp.bfloat16))


def finish_pair(mixed, ready, mid_gain, out_weight, out_gate):
    scaled = unit_channels(mixed.astype(jnp.float32), mid_gain).astype(jnp.bfloat16)
    scaled = lax.optimization_barrier(scaled)
    gate = jax.nn.sigmoid(
        jnp.einsum("ijc,cd->ijd", ready, out_gate, preferred_element_type=jnp.float32)
    )
    return (
        jnp.einsum("ijd,dc->ijc", scaled, out_weight, preferred_element_type=jnp.float32) * gate
    ).astype(jnp.bfloat16)


def per_device(pair_state, in_gain, left_weight, right_weight, mid_gain, out_weight, out_gate):
    ready, left, right = make_factors(pair_state, in_gain, left_weight, right_weight)
    count = pair_state.shape[1] * lax.axis_size("second")
    left_lines, right_lines = (
        lax.all_to_all(left, "second", split_axis=2, concat_axis=1, tiled=True),
        lax.all_to_all(right, "second", split_axis=2, concat_axis=1, tiled=True),
    )

    def meet(piece):
        return jnp.einsum("ikd,jkd->ijd", left_lines, piece, preferred_element_type=jnp.float32)

    strip = meet(lax.all_gather(right_lines, "first", axis=0, tiled=True))
    strip = (strip * count ** (-0.5)).astype(jnp.bfloat16)
    mixed = lax.all_to_all(strip, "second", split_axis=1, concat_axis=2, tiled=True)
    return finish_pair(mixed, ready, mid_gain, out_weight, out_gate)


def solution(mesh):
    in_specs = (P("first", "second", None), P(), P(), P(), P(), P(), P())
    out_specs = P("first", "second", None)
    return jax.shard_map(
        per_device, mesh=mesh, in_specs=in_specs, out_specs=out_specs, check_vma=False
    )
```

profile of v0, /device:TPU:1, one launch (start us, length us, event | category | flops | bytes accessed | tf_op | source)
XLA Modules:
  0.0 180.6 jit_solution(738637115696771919)
XLA Ops:
  6.5 1.5 convert_reduce_fusion
  8.1 1.8 fusion.13
  9.9 1.4 fusion.15
  11.3 0.8 copy-done.2
  12.1 0.3 convolution_convert_fusion.1
  12.4 1.0 copy.17
  13.4 2.4 %reshape.39 = bf16[16,2,9216]{2,1,0:T(2,128)(2,1)S(1)} reshape(bf16[128,48,48]{2,1,0:T(8,128)(2,1)S(1)} %bitcast.60) | data formatting | bytes 1179648
  15.8 28.4 %all_to_all.45 = bf16[16,2,9216]{2,1,0:T(2,128)(2,1)S(1)} all-to-all(bf16[16,2,9216]{2,1,0:T(2,128)(2,1)S(1)} %reshape.39), channel_id=1, replica_groups=mesh['first'=16,'second'=16] {'second'}, dimensions={0} | all-to-all | bytes 1179648 | tf_op jit(solution)/shard_map/all_to_all | solution.py:40
  44.2 1.5 reshape.40
  45.8 1.0 copy.19
  46.8 2.3 %all_to_all.36 = bf16[48,768,8]{1,0,2:T(8,128)(2,1)} reshape(bf16[48,16,48,8]{2,1,0,3:T(8,128)(2,1)S(1)} %copy.19) | data formatting | bytes 1179648 | tf_op jit(solution)/shard_map/all_to_all | solution.py:40
  49.1 0.3 convolution_convert_fusion
  49.4 1.0 copy.20
  50.4 2.4 %reshape.41 = bf16[16,2,9216]{2,1,0:T(2,128)(2,1)S(1)} reshape(bf16[128,48,48]{2,1,0:T(8,128)(2,1)S(1)} %bitcast.61) | data formatting | bytes 1179648
  52.8 21.8 %all_to_all.46 = bf16[16,2,9216]{2,1,0:T(2,128)(2,1)S(1)} all-to-all(bf16[16,2,9216]{2,1,0:T(2,128)(2,1)S(1)} %reshape.41), channel_id=1, replica_groups=mesh['first'=16,'second'=16] {'second'}, dimensions={0} | all-to-all | bytes 1179648 | tf_op jit(solution)/shard_map/all_to_all | solution.py:39
  74.5 1.5 reshape.42
  76.1 1.0 copy.22
  77.1 1.6 all_to_all.40
  78.7 47.9 %all-gather.2.cloned.1.call-done = bf16[768,768,8]{1,0,2:T(8,128)(2,1)} async-done(((bf16[48,768,8]{1,0,2:T(8,128)(2,1)}), bf16[768,768,8]{1,0,2:T(8,128)(2,1)}) %all-gather.2.cloned.1.call-update) | async-done | bytes 9437200 | tf_op jit(solution)/shard_map/all_gather | solution.py:46
  126.5 6.5 %fusion.12 = bf16[48,768,8]{1,0,2:T(8,128)(2,1)S(1)} fusion(bf16[768,768,8]{1,0,2:T(8,128)(2,1)} %all-gather.2.cloned.1.call-done, bf16[48,768,8]{1,0,2:T(8,128)(2,1)S(1)} %all_to_all.40), kind=kOutput, calls=%fused_computation.22 | convolution fusion | flops 453574656 | bytes 10616832 | tf_op jit(solution)/shard_map/ikd,jkd->ijd/dot_general | solution.py:44
  133.1 1.1 copy.23
  134.2 3.1 %reshape.43 = bf16[16,2,9216]{2,1,0:T(2,128)(2,1)} reshape(bf16[768,8,48]{2,1,0:T(8,128)(2,1)S(1)} %bitcast.62) | data formatting | bytes 1179648
  137.3 7.9 %all-to-all-start.2 = ((bf16[16,2,9216]{2,1,0:T(2,128)(2,1)}), bf16[16,2,9216]{2,1,0:T(2,128)(2,1)S(1)}, u32[]{:S(2)}, u32[]{:S(2)}) async-start(bf16[16,2,9216]{2,1,0:T(2,128)(2,1)} %reshape.43), calls=%async_computation.2 | async-start | bytes 1179648 | tf_op jit(solution)/shard_map/all_to_all | solution.py:48
  145.2 1.5 fusion.9
  146.7 16.8 %all-to-all-done.2 = bf16[16,2,9216]{2,1,0:T(2,128)(2,1)S(1)} async-done(((bf16[16,2,9216]{2,1,0:T(2,128)(2,1)}), bf16[16,2,9216]{2,1,0:T(2,128)(2,1)S(1)}, u32[]{:S(2)}, u32[]{:S(2)}) %all-to-all-start.2) | async-done | bytes 589856 | tf_op jit(solution)/shard_map/all_to_all | solution.py:48
  163.5 2.4 %reshape.44 = bf16[768,8,48]{2,1,0:T(8,128)(2,1)} reshape(bf16[16,2,9216]{2,1,0:T(2,128)(2,1)S(1)} %all-to-all-done.2) | data formatting | bytes 1179648
  166.0 4.1 %copy.24 = f32[48,16,48,8]{2,3,1,0:T(8,128)S(1)} copy(bf16[48,16,48,8]{0,3,2,1:T(8,128)(2,1)} %bitcast.63) | data formatting | bytes 1769472 | tf_op jit(solution)/shard_map/convert_element_type | solution.py:25
  170.0 0.4 bitcast_reduce_fusion
  170.4 0.6 fusion.4
  171.1 0.7 fusion.2
  171.8 0.5 copy-done.5
  172.4 1.4 fusion.10
  (24 shorter events, 0.1 us)
Async XLA Ops:
  6.5 5.6 %copy-start = (bf16[128,128]{1,0:T(8,128)(2,1)S(1)}, bf16[128,128]{1,0:T(8,128)(2,1)}, u32[]{:S(2)}) copy-start(bf16[128,128]{1,0:T(8,128)(2,1)} %param.10) | copy-start | bytes 98308
  6.5 3.3 %copy-start.1 = (bf16[48,48,128]{2,1,0:T(8,128)(2,1)S(1)}, bf16[48,48,128]{2,1,0:T(8,128)(2,1)}, u32[]{:S(2)}) copy-start(bf16[48,48,128]{2,1,0:T(8,128)(2,1)} %param.7) | copy-start | bytes 1769476
  6.5 120.0 %all-gather.2.cloned.1.call-start = ((), (), s32[]{:S(2)}) async-start(), calls=%async_computation.3 | async-start | bytes 10027008 | tf_op jit(solution)/shard_map/all_gather | solution.py:46
  11.3 0.8 copy-start.2
  46.8 2.3 %copy-start.3 = (bf16[48,48,128]{2,1,0:T(8,128)(2,1)S(1)}, bf16[48,48,128]{2,1,0:T(8,128)(2,1)}, u32[]{:S(2)}) copy-start(bf16[48,48,128]{2,1,0:T(8,128)(2,1)} %copy-done.2) | copy-start | bytes 1769476
  46.8 2.3 %copy-start.7 = (bf16[128,128]{1,0:T(8,128)(2,1)S(1)}, bf16[128,128]{1,0:T(8,128)(2,1)}, u32[]{:S(2)}) copy-start(bf16[128,128]{1,0:T(8,128)(2,1)} %param.9) | copy-start | bytes 98308
  134.2 11.1 %copy-start.4 = (bf16[48,48,128]{2,1,0:T(8,128)(2,1)S(1)}, bf16[48,48,128]{2,1,0:T(8,128)(2,1)}, u32[]{:S(2)}) copy-start(bf16[48,48,128]{2,1,0:T(8,128)(2,1)} %copy-done.2) | copy-start | bytes 1769476
  134.2 11.0 %copy-start.9 = (bf16[128,128]{1,0:T(8,128)(2,1)S(1)}, bf16[128,128]{1,0:T(8,128)(2,1)}, u32[]{:S(2)}) copy-start(bf16[128,128]{1,0:T(8,128)(2,1)} %param.13) | copy-start | bytes 98308
  137.3 26.3 %all-to-all-start.2 = ((bf16[16,2,9216]{2,1,0:T(2,128)(2,1)}), bf16[16,2,9216]{2,1,0:T(2,128)(2,1)S(1)}, u32[]{:S(2)}, u32[]{:S(2)}) async-start(bf16[16,2,9216]{2,1,0:T(2,128)(2,1)} %reshape.43), calls=%async_computation.2 | async-start | bytes 1179648 | tf_op jit(solution)/shard_map/all_to_all | solution.py:48
  170.4 0.7 copy-start.8
  171.1 1.3 copy-start.5
  171.1 1.3 copy-start.6
Sparse Core Ops, SparseCore 0:
  49.2 77.2 all-gather.1
where the time goes:
time: 181 us
  waiting for transfers between devices  64.7 us (36%)
  blocking collectives  50.2 us (28%)
  local copies, waits for them, and re-layouts  27.7 us (15%)
  between operations  13.7 us (8%)
  matrix products  9.99 us (6%)
  starting transfers between devices  7.95 us (4%)
  other arithmetic  6.45 us (4%)
    all_gather x1, waiting for transfers between devices, per_device(): strip = meet(lax.all_gather(right_lines, 'first', axis=0, tiled=True))  47.9 us
    all_to_all x1, blocking collectives, per_device(): lax.all_to_all(right, 'second', split_axis=2, concat_axis=1, tiled=True)  28.4 us
    all_to_all x1, blocking collectives, per_device(): lax.all_to_all(left, 'second', split_axis=2, concat_axis=1, tiled=True)  21.8 us
    all_to_all x1, waiting for transfers between devices, per_device(): lax.all_to_all(strip, 'second', split_axis=1, concat_axis=2, tiled=True)  16.8 us
    unnamed x26, local copies, waits for them, and re-layouts  14.7 us
    all_to_all x1, starting transfers between devices, per_device(): lax.all_to_all(strip, 'second', split_axis=1, concat_axis=2, tiled=True)  7.95 us
    dot_general x1, matrix products, meet(): jnp.einsum('ikd,jkd->ijd', left_lines, piece, preferred_element_type=jnp....  6.53 us
    convert_element_type x1, local copies, waits for them, and re-layouts, finish_pair(): mixed.astype(jnp.float32)  4.06 us
  transfers between devices with their start and end apart: 2, of which 2 were waited for; matrix products, arithmetic and copies ran while one was open for 4% of the time, Pallas kernels for 0%

commit v1 on v0

v1 whole, which is shorter than its diff:
```python
import functools

import jax
import jax.numpy as jnp
from jax import lax
from jax.experimental import pallas as pl
from jax.experimental.pallas import tpu as pltpu
from jax.sharding import PartitionSpec as P

MESH = pl.DeviceIdType.MESH
F32, BF16 = jnp.float32, jnp.bfloat16
VMEM = pl.BlockSpec(memory_space=pltpu.VMEM)


def norm(values, gain, axis):
    centred = values - jnp.mean(values, axis=axis, keepdims=True)
    scale = lax.rsqrt(jnp.mean(centred * centred, axis=axis, keepdims=True) + 1e-05)
    return centred * scale * gain


def place():
    a, b = lax.axis_index("first"), lax.axis_index("second")
    return a, b, a // 8, a * 8 + b // 2, lax.rem(b, 2)


def chip(c, core):
    return (c // 8, lax.rem(c, 8) * 2 + core)


def factor_rows(x_ref, gain_ref, wl_ref, wr_ref, rows_ref, msg_ref):
    weights = jnp.concatenate([wr_ref[...].astype(F32).T, wl_ref[...].astype(F32).T], axis=0)
    weights = weights.astype(BF16)
    gain = gain_ref[...]

    def tile(r, _):
        k1, i1 = r // 6, lax.rem(r, 6)
        block = x_ref[pl.ds(i1 * 8, 8), pl.ds(pl.multiple_of(k1 * 16, 16), 16), :]
        ready = norm(block.astype(F32).reshape(128, 128), gain, 1).astype(BF16)
        made = lax.dot_general(
            weights, ready, (((1,), (1,)), ((), ())), preferred_element_type=F32
        )
        rows_ref[pl.ds(r, 256, stride=24), :] = made
        return 0

    lax.fori_loop(0, 18, tile, 0)

    def pack(d, _):
        for e in range(8):
            at = d * 8 + e
            msg_ref[at] = rows_ref[pl.ds(pl.multiple_of(at * 24, 8), 24), :][:18].astype(BF16)
        return 0

    lax.fori_loop(0, 32, pack, 0)


def factor_kernel(x_ref, gain_ref, wl_ref, wr_ref, l_ref, r_ref, rows_ref, msg_ref, sems):
    a, b, half, mine, core = place()
    barrier = pltpu.get_barrier_semaphore()

    def greet(c, _):
        pl.semaphore_signal(
            barrier, inc=1, device_id=(c // 16 + 8 * core, lax.rem(c, 16)), device_id_type=MESH
        )
        return 0

    lax.fori_loop(0, 128, greet, 0)
    pl.semaphore_signal(barrier, inc=1, device_id=(a, b + 1 - 2 * core), device_id_type=MESH)
    factor_rows(x_ref, gain_ref, wl_ref, wr_ref, rows_ref, msg_ref)
    pl.semaphore_wait(barrier, 129)

    slot = lax.rem(a, 8) * 16 + b
    own = half == core

    def send(which, dest_ref, base, send_sem, recv_sem):
        def one(t, _):
            c = lax.rem(mine + t, 128)

            @pl.when(jnp.logical_or(t > 0, jnp.logical_not(own)))
            def _():
                pltpu.make_async_remote_copy(
                    src_ref=msg_ref.at[which * 128 + c],
                    dst_ref=dest_ref.at[base + slot],
                    send_sem=send_sem,
                    recv_sem=recv_sem,
                    device_id=chip(c, half),
                    device_id_type=MESH,
                ).start()

            return 0

        lax.fori_loop(0, 128, one, 0)

        @pl.when(own)
        def _():
            dest_ref[base + slot] = msg_ref[which * 128 + mine]

    def settle(ref, sem):
        @pl.when(own)
        def _():
            view = ref.at[pl.ds(0, 127)]
            pltpu.make_async_copy(view, view, sem).wait()

        @pl.when(jnp.logical_not(own))
        def _():
            view = ref.at[pl.ds(0, 128)]
            pltpu.make_async_copy(view, view, sem).wait()

    send(0, r_ref, half * 128, sems.at[0], sems.at[1])
    send(1, l_ref, 0, sems.at[2], sems.at[3])
    settle(r_ref, sems.at[1])
    swap = pltpu.make_async_remote_copy(
        src_ref=r_ref.at[pl.ds(core * 128, 128)],
        dst_ref=r_ref.at[pl.ds(core * 128, 128)],
        send_sem=sems.at[4],
        recv_sem=sems.at[5],
        device_id=(a, b + 1 - 2 * core),
        device_id_type=MESH,
    )
    swap.start()
    settle(l_ref, sems.at[3])
    swap.wait()
    settle(msg_ref, sems.at[0])
    settle(msg_ref, sems.at[2])


def product_rows(l_ref, r_ref, c_ref, pad_ref, rk_ref, lf_ref, lb_ref, z_ref, g_ref):
    lane = lax.broadcasted_iota(jnp.int32, (64, 128), 1)

    def quarter(h, _):
        groups = []
        for bb in range(8):
            b = h * 8 + bb
            for ja in range(16):
                pad_ref[ja, 0:18, :] = r_ref[ja * 16 + b].astype(F32)
            for k1 in range(3):
                block = pad_ref[:, k1 * 6 : k1 * 6 + 8, :].reshape(128, 128).T
                at = pl.multiple_of(b * 48 + k1 * 16, 16)
                for j0 in range(8):
                    rk_ref[pl.ds(at, 16), j0 * 128 : (j0 + 1) * 128] = block[
                        j0 * 16 : (j0 + 1) * 16
                    ].astype(BF16)
        for bb in range(8):
            b = h * 8 + bb
            for ia in range(8):
                pad_ref[ia, 0:18, :] = l_ref[ia * 16 + b].astype(F32)
            for k1 in range(3):
                groups.append(pad_ref[0:8, k1 * 6 : k1 * 6 + 8, :].reshape(64, 128))
            while len(groups) >= 8:
                blocks, groups = groups[:8], groups[8:]
                for bit in (1, 2, 4):
                    high = (lane // (16 * bit)) % 2 == 1
                    turned = list(blocks)
                    for n in range(8):
                        if n & bit:
                            continue
                        one, two = blocks[n], blocks[n + bit]
                        turned[n] = jnp.where(high, pltpu.roll(two, 16 * bit, 1), one)
                        turned[n + bit] = jnp.where(high, two, pltpu.roll(one, 128 - 16 * bit, 1))
                    blocks = turned
                tile = bb * 3 // 8
                for i0 in range(8):
                    for ia in range(8):
                        lf_ref[
                            pl.ds((h * 3 + tile) * 384 + ia * 48 + i0, 6, stride=8), :
                        ] = blocks[i0][ia * 8 : ia * 8 + 6]
        return 0

    lax.fori_loop(0, 2, quarter, 0)
    for tile in range(6):
        lb_ref[:, tile * 128 : (tile + 1) * 128] = lf_ref[
            tile * 384 : (tile + 1) * 384, :
        ].astype(BF16)
    for n in range(4):
        made = jnp.dot(
            lb_ref[...], rk_ref[:, n * 256 : (n + 1) * 256], preferred_element_type=F32
        )
        made = made * 768**-0.5
        z_ref[pl.ds(2 * n, 384, stride=8), :] = made[:, :128]
        z_ref[pl.ds(2 * n + 1, 384, stride=8), :] = made[:, 128:]

    def give(ia, _):
        for ih in range(3):
            at = pl.multiple_of((ia * 3 + ih) * 128, 128)
            block = z_ref[pl.ds(at, 128), :].T
            for jb in range(16):
                g_ref[jb, ih * 6 : ih * 6 + 6, :] = block[jb * 8 : jb * 8 + 6]
        for jb in range(16):
            c_ref[ia * 16 + jb] = g_ref[jb][:18].astype(BF16)
        return 0

    lax.fori_loop(0, 8, give, 0)


def return_kernel(c_ref, d_ref, sems):
    a, b, half, mine, core = place()
    barrier = pltpu.get_barrier_semaphore()

    def greet(c, _):
        pl.semaphore_signal(barrier, inc=1, device_id=chip(c, half), device_id_type=MESH)
        return 0

    lax.fori_loop(0, 128, greet, 0)
    pl.semaphore_wait(barrier, 128)
    own = half == core
    home = lax.rem(a, 8) * 16 + b

    def one(t, _):
        s = lax.rem(home + t, 128)

        @pl.when(jnp.logical_or(t > 0, jnp.logical_not(own)))
        def _():
            pltpu.make_async_remote_copy(
                src_ref=c_ref.at[s],
                dst_ref=d_ref.at[mine],
                send_sem=sems.at[0],
                recv_sem=sems.at[1],
                device_id=(core * 8 + s // 16, lax.rem(s, 16)),
                device_id_type=MESH,
            ).start()

        return 0

    lax.fori_loop(0, 128, one, 0)

    @pl.when(own)
    def _():
        d_ref[mine] = c_ref[home]

    for sem in (sems.at[0], sems.at[1]):

        @pl.when(own)
        def _():
            view = d_ref.at[pl.ds(0, 127)]
            pltpu.make_async_copy(view, view, sem).wait()

        @pl.when(jnp.logical_not(own))
        def _():
            view = d_ref.at[pl.ds(0, 128)]
            pltpu.make_async_copy(view, view, sem).wait()


def finish_kernel(
    d_ref, x_ref, in_gain_ref, mid_gain_ref, w_ref, wg_ref, out_ref, rows_ref
):
    def spread(d, _):
        for e in range(8):
            at = d * 8 + e
            rows_ref[pl.ds(pl.multiple_of(at * 24, 8), 18), :] = d_ref[at].astype(F32)
        return 0

    lax.fori_loop(0, 16, spread, 0)
    column = jnp.broadcast_to(mid_gain_ref[...], (128, 128)).T

    def tile(n, _):
        ih, jp = n // 3, lax.rem(n, 3)
        i_at, j_at = pl.ds(ih * 16, 16), pl.ds(pl.multiple_of(jp * 16, 16), 16)
        block = x_ref[i_at, j_at, :].astype(F32).reshape(256, 128)
        ready = norm(block, in_gain_ref[...], 1).astype(BF16)
        gate = jax.nn.sigmoid(jnp.dot(ready, wg_ref[...], preferred_element_type=F32))
        halves = []
        for e in range(2):
            mixed = rows_ref[pl.ds(ih * 6 + jp * 2 + e, 128, stride=24), :]
            scaled = norm(mixed, column, 0).T.astype(BF16)
            made = jnp.dot(scaled, w_ref[...], preferred_element_type=F32)
            halves.append(made.reshape(16, 8, 128))
        made = jnp.concatenate(halves, axis=1)
        out_ref[i_at, j_at, :] = (made * gate.reshape(16, 16, 128)).astype(BF16)
        return 0

    lax.fori_loop(0, 9, tile, 0)


def per_device(pair_state, in_gain, left_weight, right_weight, mid_gain, out_weight, out_gate):
    def shape(*s, t=BF16):
        return jax.ShapeDtypeStruct(s, t)

    in_row, mid_row = in_gain.reshape(1, 128), mid_gain.reshape(1, 128)
    left, right = pl.pallas_call(
        factor_kernel,
        name="factors",
        out_shape=(shape(128, 18, 128), shape(256, 18, 128)),
        in_specs=[VMEM] * 4,
        out_specs=(VMEM, VMEM),
        scratch_shapes=[
            pltpu.VMEM((256 * 24, 128), F32),
            pltpu.VMEM((256, 18, 128), BF16),
            pltpu.SemaphoreType.DMA((6,)),
        ],
        compiler_params=pltpu.CompilerParams(collective_id=1, has_side_effects=True),
    )(pair_state, in_row, left_weight, right_weight)
    products = pl.pallas_call(
        product_rows,
        name="products",
        out_shape=shape(128, 18, 128),
        in_specs=[VMEM] * 2,
        out_specs=VMEM,
        scratch_shapes=[
            pltpu.VMEM((16, 24, 128), F32),
            pltpu.VMEM((768, 1024), BF16),
            pltpu.VMEM((6 * 384, 128), F32),
            pltpu.VMEM((384, 768), BF16),
            pltpu.VMEM((3072, 128), F32),
            pltpu.VMEM((16, 24, 128), F32),
        ],
    )(left, right)
    mixed = pl.pallas_call(
        return_kernel,
        name="returns",
        out_shape=shape(128, 18, 128),
        in_specs=[VMEM],
        out_specs=VMEM,
        scratch_shapes=[pltpu.SemaphoreType.DMA((2,))],
        compiler_params=pltpu.CompilerParams(collective_id=2, has_side_effects=True),
    )(products)
    return pl.pallas_call(
        finish_kernel,
        name="finish",
        out_shape=shape(48, 48, 128),
        in_specs=[VMEM] * 6,
        out_specs=VMEM,
        scratch_shapes=[
            pltpu.VMEM((128 * 24, 128), F32),
        ],
    )(mixed, pair_state, in_row, mid_row, out_weight, out_gate)


def solution(mesh):
    in_specs = (P("first", "second", None), P(), P(), P(), P(), P(), P())
    out_specs = P("first", "second", None)
    return jax.shard_map(
        per_device, mesh=mesh, in_specs=in_specs, out_specs=out_specs, check_vma=False
    )
```

time: 181 us -> 100 us (0.55)
  Pallas kernels: 0 us -> 100 us
  waiting for transfers between devices: 64.7 us -> 0 us
  blocking collectives: 50.2 us -> 0 us
  local copies, waits for them, and re-layouts: 27.7 us -> 0 us
  between operations: 13.7 us -> 0.02 us
  matrix products: 9.99 us -> 0 us
  starting transfers between devices: 7.95 us -> 0 us
  other arithmetic: 6.45 us -> 0 us
    pallas_call x0 -> x4, Pallas kernels: none -> 100 us  [the longest x1 49.1 us: per_device(): pl.pallas_call(factor_kernel, name='factors', out_shape=(shape(128, 18, 1...]
    all_to_all x2 -> x0, blocking collectives: 50.2 us -> none  [the longest x1 28.4 us: per_device(): lax.all_to_all(right, 'second', split_axis=2, concat_axis=1, tiled=True)]
    all_gather x1 -> x0, waiting for transfers between devices: 47.9 us -> none  [per_device(): strip = meet(lax.all_gather(right_lines, 'first', axis=0, tiled=True))]
    all_to_all x1 -> x0, waiting for transfers between devices: 16.8 us -> none  [per_device(): lax.all_to_all(strip, 'second', split_axis=1, concat_axis=2, tiled=True)]
    unnamed x26 -> x0, local copies, waits for them, and re-layouts: 14.7 us -> none
    dot_general x5 -> x0, matrix products: 9.99 us -> none  [the longest x1 6.53 us: meet(): jnp.einsum('ikd,jkd->ijd', left_lines, piece, preferred_element_type=jnp....]
    all_to_all x1 -> x0, starting transfers between devices: 7.95 us -> none  [per_device(): lax.all_to_all(strip, 'second', split_axis=1, concat_axis=2, tiled=True)]
    convert_element_type x4 -> x0, local copies, waits for them, and re-layouts: 7.08 us -> none  [the longest x1 4.06 us: finish_pair(): mixed.astype(jnp.float32)]
  transfers between devices with their start and end apart: 2 -> 0, of which waited for: 2 -> 0; matrix products, arithmetic and copies ran while one was open for 4% -> 0% of each run, Pallas kernels for 0% -> 0%
where the time goes in v1:
time: 100 us
  Pallas kernels  100 us (100%)
    pallas_call x1, Pallas kernels, per_device(): pl.pallas_call(factor_kernel, name='factors', out_shape=(shape(128, 18, 1...  49.1 us
    pallas_call x1, Pallas kernels, per_device(): pl.pallas_call(return_kernel, name='returns', out_shape=shape(128, 18, 12...  38.1 us
    pallas_call x1, Pallas kernels, per_device(): pl.pallas_call(product_rows, name='products', out_shape=shape(128, 18, 12...  7.07 us
    pallas_call x1, Pallas kernels, per_device(): pl.pallas_call(finish_kernel, name='finish', out_shape=shape(48, 48, 128)...  5.81 us

profile of v1, /device:TPU:1, one launch (start us, length us, event | category | flops | bytes accessed | tf_op | source)
XLA Modules:
  0.0 100.1 jit_solution(7207014959514348870)
XLA Ops:
  0.0 49.1 %factors.1 = (bf16[128,18,128]{2,1,0:T(8,128)(2,1)}, bf16[256,18,128]{2,1,0:T(8,128)(2,1)}) custom-call(bf16[48,48,128]{2,1,0:T(8,128)(2,1)} %x_ref.3, f32[1,128]{1,0:T(1,128)} %bitcast.2, bf16[128,128]{1,0:T(8,128)(2,1)} %wl_ref.1, bf16[128,128]{1,0:T(8,128)(2,1)} %wr_ref.1), custom_call_target="tpu_custom_call" | custom-call | tf_op jit(solution)/shard_map/factors/pallas_call | solution.py:278
  49.1 7.1 %products.1.c_ref = bf16[128,18,128]{2,1,0:T(8,128)(2,1)} custom-call(bf16[128,18,128]{2,1,0:T(8,128)(2,1)} %get-tuple-element.7.l_ref, bf16[256,18,128]{2,1,0:T(8,128)(2,1)} %get-tuple-element.8.r_ref), custom_call_target="tpu_custom_call" | custom-call | tf_op jit(solution)/shard_map/products/pallas_call | solution.py:291
  56.2 38.1 %returns.1.d_ref = bf16[128,18,128]{2,1,0:T(8,128)(2,1)} custom-call(bf16[128,18,128]{2,1,0:T(8,128)(2,1)} %products.1.c_ref), custom_call_target="tpu_custom_call" | custom-call | tf_op jit(solution)/shard_map/returns/pallas_call | solution.py:306
  94.3 5.8 %finish.1 = bf16[48,48,128]{2,1,0:T(8,128)(2,1)} custom-call(bf16[128,18,128]{2,1,0:T(8,128)(2,1)} %returns.1.d_ref, bf16[48,48,128]{2,1,0:T(8,128)(2,1)} %x_ref.3, f32[1,128]{1,0:T(1,128)} %bitcast.3, f32[1,128]{1,0:T(1,128)} %bitcast.4, bf16[128,128]{1,0:T(8,128)(2,1)} %w_ref.1, bf16[128,128]{1,0:T(8,128)(2,1)} %wg_ref.1), custom_call_target="tpu_custom_call" | custom-call | tf_op jit(solution)/shard_map/finish/pallas_call | solution.py:315

commit v2 on v0

v2 whole, which is shorter than its diff:
```python
import jax
import jax.numpy as jnp
from jax import lax
from jax.experimental import pallas as pl
from jax.experimental.pallas import tpu as pltpu
from jax.sharding import PartitionSpec as P

LOGICAL = pl.DeviceIdType.LOGICAL
F32, BF16 = jnp.float32, jnp.bfloat16
VMEM = pl.BlockSpec(memory_space=pltpu.VMEM)
NT = (((1,), (1,)), ((), ()))


def norm(values, gain, axis):
    centred = values - jnp.mean(values, axis=axis, keepdims=True)
    scale = lax.rsqrt(jnp.mean(centred * centred, axis=axis, keepdims=True) + 1e-05)
    return centred * scale * gain


def around(start, step, unroll=8):
    def at(t):
        c = start + t
        step(jnp.where(c >= 128, c - 128, c))

    def some(n, _):
        for e in range(unroll):
            at(n * unroll + e + 1)
        return 0

    lax.fori_loop(0, 127 // unroll, some, 0)
    for t in range(127 // unroll * unroll + 1, 128):
        at(jnp.int32(t))


def make_right(x_ref, gain_ref, w_ref, ready_ref, rows_ref, msg_ref):
    gain = gain_ref[...]
    weights = w_ref[...].astype(F32).T.astype(BF16)

    def tiles(k1, _):
        for i1 in range(6):
            block = x_ref[i1 * 8 : i1 * 8 + 8, pl.ds(pl.multiple_of(k1 * 16, 16), 16), :]
            ready = norm(block.astype(F32).reshape(128, 128), gain, 1).astype(BF16)
            ready_ref[k1 * 6 + i1] = ready
            made = lax.dot_general(weights, ready, NT, preferred_element_type=F32)
            rows_ref[pl.ds(k1 * 6 + i1, 128, stride=18), :] = made
        return 0

    lax.fori_loop(0, 3, tiles, 0)

    def pack(n, _):
        rows = rows_ref[pl.ds(pl.multiple_of(n * 288, 8), 288), :]
        msg_ref[pl.ds(n * 144, 144)] = rows.astype(BF16).reshape(144, 2, 128)
        return 0

    lax.fori_loop(0, 8, pack, 0)


def make_left(w_ref, ready_ref, rows_ref, msg_ref):
    weights = w_ref[...].astype(F32).T.astype(BF16)

    def tiles(k1, _):
        for i1 in range(6):
            made = lax.dot_general(
                weights, ready_ref[k1 * 6 + i1], NT, preferred_element_type=F32
            )
            at = (i1 // 2) * 768 + k1 * 2 + i1 % 2
            rows_ref[pl.ds(at, 128, stride=6), :] = made
        return 0

    lax.fori_loop(0, 3, tiles, 0)
    for ih in range(3):

        def pack(n, _):
            rows = rows_ref[pl.ds(pl.multiple_of(ih * 768 + n * 192, 8), 192), :]
            msg_ref[ih, pl.ds(n * 96, 96)] = rows.astype(BF16).reshape(96, 2, 128)
            return 0

        lax.fori_loop(0, 4, pack, 0)


def make_gate(w_ref, ready_ref, gate_ref):
    weights = w_ref[...]

    def tiles(k1, _):
        for i1 in range(6):
            made = jnp.dot(ready_ref[k1 * 6 + i1], weights, preferred_element_type=F32)
            gate = jax.nn.sigmoid(made).reshape(8, 16, 128)
            gate_ref[i1 * 8 : i1 * 8 + 8, pl.ds(pl.multiple_of(k1 * 16, 16), 16), :] = gate
        return 0

    lax.fori_loop(0, 3, tiles, 0)


def turn_right(in_ref, pad_ref, right_ref):
    def lines(n, _):
        for e in range(2):
            b = n * 2 + e
            pad_ref[e, 0:288, :] = in_ref[b].reshape(288, 128).astype(F32)
            for k1 in range(3):
                parts = [pad_ref[e, ja * 18 + k1 * 6 : ja * 18 + k1 * 6 + 8, :] for ja in range(16)]
                block = jnp.concatenate(parts, axis=0).T.astype(BF16)
                at = pl.multiple_of(b * 48 + k1 * 16, 16)
                for j0 in range(8):
                    right_ref[pl.ds(at, 16), j0 * 128 : j0 * 128 + 128] = block[
                        j0 * 16 : j0 * 16 + 16
                    ]
        return 0

    lax.fori_loop(0, 8, lines, 0)


def turn_left(ih, in_ref, rows_ref, left_ref):
    rows_ref[0:768, :] = in_ref[ih].reshape(768, 128).astype(F32)
    lane = lax.broadcasted_iota(jnp.int32, (8, 128), 1)
    highs = {bit: (lane // (16 * bit)) % 2 == 1 for bit in (1, 2, 4)}
    for tile in range(6):
        for il in range(2):
            blocks = []
            for q in range(tile * 8, tile * 8 + 8):
                at = (q // 3) * 48 + (q % 3) * 2 + il
                blocks.append(rows_ref[pl.ds(at, 8, stride=6), :])
            for bit in (1, 2, 4):
                turned = list(blocks)
                for n in range(8):
                    if n & bit:
                        continue
                    one, two = blocks[n], blocks[n + bit]
                    turned[n] = jnp.where(highs[bit], pltpu.roll(two, 16 * bit, 1), one)
                    turned[n + bit] = jnp.where(
                        highs[bit], two, pltpu.roll(one, 128 - 16 * bit, 1)
                    )
                blocks = turned
            for i0 in range(0, 8, 2):
                at = (il * 8 + i0) * 8
                left_ref[at : at + 16, tile * 128 : tile * 128 + 128] = jnp.concatenate(
                    blocks[i0 : i0 + 2], axis=0
                ).astype(BF16)


def multiply(ih, left_ref, right_ref, z_ref, rows_ref, msg_ref):
    for n in range(4):
        made = jnp.dot(
            left_ref[...], right_ref[:, n * 256 : n * 256 + 256], preferred_element_type=F32
        )
        made = made * 768**-0.5
        for e in range(2):
            for i16 in range(16):
                z_ref[pl.ds(i16 * 8 + n * 2 + e, 8, stride=136), :] = made[
                    i16 * 8 : i16 * 8 + 8, e * 128 : e * 128 + 128
                ]
    for ia in range(8):
        block = z_ref[ia * 136 : ia * 136 + 128, :].T
        for jb in range(16):
            at = (ia * 16 + jb) * 6
            rows_ref[at : at + 6, :] = block[jb * 8 : jb * 8 + 6]
    for n in range(4):
        rows = rows_ref[n * 192 : n * 192 + 192, :]
        msg_ref[ih, n * 96 : n * 96 + 96] = rows.astype(BF16).reshape(96, 2, 128)


def finish(ih, in_ref, column, w_ref, gate_ref, rows_ref, out_ref):
    rows_ref[0:768, :] = in_ref[ih].reshape(768, 128).astype(F32)
    i_at = pl.ds(ih * 16, 16)
    for jp in range(3):
        halves = []
        for e in range(2):
            mixed = rows_ref[pl.ds(jp * 2 + e, 128, stride=6), :]
            scaled = norm(mixed, column, 0).T.astype(BF16)
            made = jnp.dot(scaled, w_ref[...], preferred_element_type=F32)
            halves.append(made.reshape(16, 8, 128))
        made = jnp.concatenate(halves, axis=1) * gate_ref[i_at, jp * 16 : jp * 16 + 16, :]
        out_ref[i_at, jp * 16 : jp * 16 + 16, :] = made.astype(BF16)


def kernel(
    x_ref, in_gain_ref, wl_ref, wr_ref, mid_gain_ref, wo_ref, wg_ref, out_ref,
    ready_ref, gate_ref, rows_ref, rmsg_ref, lmsg_ref, rin_ref, lin_ref, pad_ref,
    right_ref, left_ref, z_ref, cmsg_ref, cin_ref, send, recv,
):
    a, b = lax.axis_index("first"), lax.axis_index("second")
    half, mine, core = a // 8, a * 8 + b // 2, lax.rem(b, 2)
    home = lax.rem(a, 8) * 16 + b
    own = half == core
    partner = a * 16 + b + 1 - 2 * core
    barrier = pltpu.get_barrier_semaphore()

    def greet(c):
        pl.semaphore_signal(barrier, inc=1, device_id=core * 128 + c, device_id_type=LOGICAL)

    def copy(src, dst, n, device):
        return pltpu.make_async_remote_copy(
            src_ref=src,
            dst_ref=dst,
            send_sem=send.at[n],
            recv_sem=recv.at[n],
            device_id=device,
            device_id_type=LOGICAL,
        )

    def spread(start, n, src, dst, device, keep):
        around(start, lambda c: copy(src(c), dst, n, device(c)).start())

        @pl.when(jnp.logical_not(own))
        def _():
            copy(src(start), dst, n, device(start)).start()

        @pl.when(own)
        def _():
            keep()

    def settle(ref, rows, sem):
        @pl.when(own)
        def _():
            view = ref.at[pl.ds(0, 127 * rows)]
            pltpu.make_async_copy(view, view, sem).wait()

        @pl.when(jnp.logical_not(own))
        def _():
            view = ref.at[pl.ds(0, 128 * rows)]
            pltpu.make_async_copy(view, view, sem).wait()

    around(home, greet)
    greet(home)
    pl.semaphore_signal(barrier, inc=1, device_id=partner, device_id_type=LOGICAL)
    make_right(x_ref, in_gain_ref, wr_ref, ready_ref, rows_ref, rmsg_ref)
    pl.semaphore_wait(barrier, 129)

    def keep_right():
        rin_ref[b, pl.ds(a * 9, 9)] = rmsg_ref[pl.ds(mine * 9, 9)]

    spread(
        mine,
        0,
        lambda c: rmsg_ref.at[pl.ds(c * 9, 9)],
        rin_ref.at[b, pl.ds(a * 9, 9)],
        lambda c: c * 2 + half,
        keep_right,
    )
    make_left(wl_ref, ready_ref, rows_ref, lmsg_ref)
    slot = b * 8 + lax.rem(a, 8)
    for ih in range(3):

        def keep_left():
            lin_ref[ih, pl.ds(slot * 3, 3)] = lmsg_ref[ih, pl.ds(mine * 3, 3)]

        spread(
            mine,
            1 + ih,
            lambda c: lmsg_ref.at[ih, pl.ds(c * 3, 3)],
            lin_ref.at[ih, pl.ds(slot * 3, 3)],
            lambda c: c * 2 + half,
            keep_left,
        )
    make_gate(wg_ref, ready_ref, gate_ref)
    settle(rmsg_ref, 9, recv.at[0])
    lines = rin_ref.at[:, pl.ds(core * 72, 72)]
    swap = copy(lines, lines, 7, partner)
    swap.start()
    swap.wait()
    turn_right(rin_ref, pad_ref, right_ref)
    for ih in range(3):
        settle(lmsg_ref.at[0], 3, recv.at[1 + ih])
        turn_left(ih, lin_ref, rows_ref, left_ref)
        multiply(ih, left_ref, right_ref, z_ref, rows_ref, cmsg_ref)

        def keep_product():
            cin_ref[ih, pl.ds(mine * 3, 3)] = cmsg_ref[ih, pl.ds(home * 3, 3)]

        spread(
            home,
            4 + ih,
            lambda c: cmsg_ref.at[ih, pl.ds(c * 3, 3)],
            cin_ref.at[ih, pl.ds(mine * 3, 3)],
            lambda c: core * 128 + c,
            keep_product,
        )
    column = jnp.broadcast_to(mid_gain_ref[...], (128, 128)).T
    for ih in range(3):
        settle(cmsg_ref.at[0], 3, recv.at[4 + ih])
        finish(ih, cin_ref, column, wo_ref, gate_ref, rows_ref, out_ref)
    settle(rmsg_ref, 9, send.at[0])
    for n in range(1, 7):
        settle(cmsg_ref.at[0], 3, send.at[n])


def per_device(pair_state, in_gain, left_weight, right_weight, mid_gain, out_weight, out_gate):
    return pl.pallas_call(
        kernel,
        name="triangle",
        out_shape=jax.ShapeDtypeStruct((48, 48, 128), BF16),
        in_specs=[VMEM] * 7,
        out_specs=VMEM,
        scratch_shapes=[
            pltpu.VMEM((18, 128, 128), BF16),
            pltpu.VMEM((48, 48, 128), F32),
            pltpu.VMEM((2304, 128), F32),
            pltpu.VMEM((1152, 2, 128), BF16),
            pltpu.VMEM((3, 384, 2, 128), BF16),
            pltpu.VMEM((16, 144, 2, 128), BF16),
            pltpu.VMEM((3, 384, 2, 128), BF16),
            pltpu.VMEM((2, 296, 128), F32),
            pltpu.VMEM((768, 1024), BF16),
            pltpu.VMEM((128, 768), BF16),
            pltpu.VMEM((8 * 136, 128), F32),
            pltpu.VMEM((3, 384, 2, 128), BF16),
            pltpu.VMEM((3, 384, 2, 128), BF16),
            pltpu.SemaphoreType.DMA((8,)),
            pltpu.SemaphoreType.DMA((8,)),
        ],
        compiler_params=pltpu.CompilerParams(collective_id=1, has_side_effects=True),
    )(
        pair_state,
        in_gain.reshape(1, 128),
        left_weight,
        right_weight,
        mid_gain.reshape(1, 128),
        out_weight,
        out_gate,
    )


def solution(mesh):
    in_specs = (P("first", "second", None), P(), P(), P(), P(), P(), P())
    out_specs = P("first", "second", None)
    return jax.shard_map(
        per_device, mesh=mesh, in_specs=in_specs, out_specs=out_specs, check_vma=False
    )
```

time: 181 us -> 60.9 us (0.34)
  waiting for transfers between devices: 64.7 us -> 0 us
  Pallas kernels: 0 us -> 58.8 us
  blocking collectives: 50.2 us -> 0 us
  local copies, waits for them, and re-layouts: 27.7 us -> 1.92 us
  between operations: 13.7 us -> 0.01 us
  matrix products: 9.99 us -> 0 us
  starting transfers between devices: 7.95 us -> 0 us
  other arithmetic: 6.45 us -> 0 us
    pallas_call x0 -> x1, Pallas kernels: none -> 58.8 us  [per_device(): pl.pallas_call(kernel, name='triangle', out_shape=jax.ShapeDtypeStruct((4...]
    all_to_all x2 -> x0, blocking collectives: 50.2 us -> none  [the longest x1 28.4 us: per_device(): lax.all_to_all(right, 'second', split_axis=2, concat_axis=1, tiled=True)]
    all_gather x1 -> x0, waiting for transfers between devices: 47.9 us -> none  [per_device(): strip = meet(lax.all_gather(right_lines, 'first', axis=0, tiled=True))]
    all_to_all x1 -> x0, waiting for transfers between devices: 16.8 us -> none  [per_device(): lax.all_to_all(strip, 'second', split_axis=1, concat_axis=2, tiled=True)]
    unnamed x26 -> x1, local copies, waits for them, and re-layouts: 14.7 us -> 1.92 us
    dot_general x5 -> x0, matrix products: 9.99 us -> none  [the longest x1 6.53 us: meet(): jnp.einsum('ikd,jkd->ijd', left_lines, piece, preferred_element_type=jnp....]
    all_to_all x1 -> x0, starting transfers between devices: 7.95 us -> none  [per_device(): lax.all_to_all(strip, 'second', split_axis=1, concat_axis=2, tiled=True)]
    convert_element_type x4 -> x0, local copies, waits for them, and re-layouts: 7.08 us -> none  [the longest x1 4.06 us: finish_pair(): mixed.astype(jnp.float32)]
  transfers between devices with their start and end apart: 2 -> 0, of which waited for: 2 -> 0; matrix products, arithmetic and copies ran while one was open for 4% -> 0% of each run, Pallas kernels for 0% -> 0%
where the time goes in v2:
time: 60.9 us; the launch traced here: 60.7 us
  Pallas kernels  58.8 us (97%)
  local copies, waits for them, and re-layouts  1.92 us (3%)
    pallas_call x1, Pallas kernels, per_device(): pl.pallas_call(kernel, name='triangle', out_shape=jax.ShapeDtypeStruct((4...  58.8 us
    unnamed x1, local copies, waits for them, and re-layouts  1.92 us

profile of v2, /device:TPU:1, one launch (start us, length us, event | category | flops | bytes accessed | tf_op | source)
XLA Modules:
  0.0 60.7 jit_solution(18212797782777668819)
XLA Ops:
  0.0 58.8 %triangle.1 = bf16[48,48,128]{2,1,0:T(8,128)(2,1)} custom-call(bf16[48,48,128]{2,1,0:T(8,128)(2,1)} %x_ref.1, f32[1,128]{1,0:T(1,128)} %bitcast.2, bf16[128,128]{1,0:T(8,128)(2,1)} %wl_ref.1, bf16[128,128]{1,0:T(8,128)(2,1)} %wr_ref.1, f32[1,128]{1,0:T(1,128)} %bitcast.3, bf16[128,128]{1,0:T(8,128)(2,1)} %wo_ref.1, bf16[128,128]{1,0:T(8,128)(2,1)} %wg_ref.1), custom_call_target="tpu_custom_call" | custom-call | tf_op jit(solution)/shard_map/triangle/pallas_call | solution.py:287
  58.8 1.9 %copy.9 = bf16[48,48,128]{2,1,0:T(8,128)(2,1)} copy(bf16[48,48,128]{2,1,0:T(8,128)(2,1)} %triangle.1) | data formatting | bytes 1179648

commit v3 on v2

--- a/solution.py
+++ b/solution.py
@@ -17,19 +17,25 @@
     return centred * scale * gain
 
 
-def around(start, step, unroll=8):
-    def at(t):
-        c = start + t
-        step(jnp.where(c >= 128, c - 128, c))
-
-    def some(n, _):
-        for e in range(unroll):
-            at(n * unroll + e + 1)
-        return 0
-
-    lax.fori_loop(0, 127 // unroll, some, 0)
-    for t in range(127 // unroll * unroll + 1, 128):
-        at(jnp.int32(t))
+FAR_FIRST = [(dy, dx) for dy in (2, 1, 3, 0) for dx in (2, 1, 3, 0)]
+
+
+def ring(at, by, size):
+    return jnp.where(at + by >= size, at + by - size, at + by)
+
+
+def outward(z, lines, step, last):
+    def plane(n, _):
+        m = (n + 1) // 2
+        there = ring(z, jnp.where(n % 2 == 0, 4 + m, 4 - m), 8)
+        for line in lines:
+            step(line, there)
+        return 0
+
+    lax.fori_loop(0, 7, plane, 0)
+    for line in lines[:-1]:
+        step(line, z)
+    last()
 
 
 def make_right(x_ref, gain_ref, w_ref, ready_ref, rows_ref, msg_ref):
@@ -173,19 +179,40 @@
 
 
 def kernel(
-    x_ref, in_gain_ref, wl_ref, wr_ref, mid_gain_ref, wo_ref, wg_ref, out_ref,
+    x_hbm, in_gain_hbm, wl_hbm, wr_hbm, mid_gain_hbm, wo_hbm, wg_hbm, out_ref,
+    x_ref, in_gain_ref, wl_ref, wr_ref, mid_gain_ref, wo_ref, wg_ref,
     ready_ref, gate_ref, rows_ref, rmsg_ref, lmsg_ref, rin_ref, lin_ref, pad_ref,
-    right_ref, left_ref, z_ref, cmsg_ref, cin_ref, send, recv,
+    right_ref, left_ref, z_ref, cmsg_ref, cin_ref, load, send, recv,
 ):
+    hbm = (x_hbm, in_gain_hbm, wr_hbm, wl_hbm, mid_gain_hbm, wo_hbm, wg_hbm)
+    vmem = (x_ref, in_gain_ref, wr_ref, wl_ref, mid_gain_ref, wo_ref, wg_ref)
+    loads = [pltpu.make_async_copy(s, d, load.at[n]) for n, (s, d) in enumerate(zip(hbm, vmem))]
+    for one in loads:
+        one.start()
     a, b = lax.axis_index("first"), lax.axis_index("second")
-    half, mine, core = a // 8, a * 8 + b // 2, lax.rem(b, 2)
+    y, x, z, core = a // 4, lax.rem(a, 4), b // 2, lax.rem(b, 2)
+    half, mine = a // 8, a * 8 + z
     home = lax.rem(a, 8) * 16 + b
     own = half == core
     partner = a * 16 + b + 1 - 2 * core
     barrier = pltpu.get_barrier_semaphore()
 
-    def greet(c):
-        pl.semaphore_signal(barrier, inc=1, device_id=core * 128 + c, device_id_type=LOGICAL)
+    out_lines = [ring(y, dy, 4) * 4 + ring(x, dx, 4) for dy, dx in FAR_FIRST]
+    near = lax.rem(y, 2)
+    back_lines = [
+        (ya * 4 + ring(x, dx, 4), c)
+        for ya in (1 - near, near)
+        for dx in (2, 1, 3, 0)
+        for c in (1 - core, core)
+    ]
+
+    def greet(line, there):
+        pl.semaphore_signal(
+            barrier,
+            inc=1,
+            device_id=core * 128 + line[0] * 16 + there * 2 + line[1],
+            device_id_type=LOGICAL,
+        )
 
     def copy(src, dst, n, device):
         return pltpu.make_async_remote_copy(
@@ -197,16 +224,32 @@
             device_id_type=LOGICAL,
         )
 
-    def spread(start, n, src, dst, device, keep):
-        around(start, lambda c: copy(src(c), dst, n, device(c)).start())
-
-        @pl.when(jnp.logical_not(own))
-        def _():
-            copy(src(start), dst, n, device(start)).start()
-
-        @pl.when(own)
-        def _():
-            keep()
+    def spread(n, lines, index, device, src, dst, keep):
+        def step(line, there):
+            copy(src(index(line, there)), dst, n, device(line, there)).start()
+
+        def last():
+            @pl.when(jnp.logical_not(own))
+            def _():
+                step(lines[-1], z)
+
+            @pl.when(own)
+            def _():
+                keep()
+
+        outward(z, lines, step, last)
+
+    def out_index(line, there):
+        return line * 8 + there
+
+    def out_device(line, there):
+        return line * 16 + there * 2 + half
+
+    def back_index(line, there):
+        return line[0] * 16 + there * 2 + line[1]
+
+    def back_device(line, there):
+        return core * 128 + back_index(line, there)
 
     def settle(ref, rows, sem):
         @pl.when(own)
@@ -219,9 +262,10 @@
             view = ref.at[pl.ds(0, 128 * rows)]
             pltpu.make_async_copy(view, view, sem).wait()
 
-    around(home, greet)
-    greet(home)
+    outward(z, back_lines, greet, lambda: greet(back_lines[-1], z))
     pl.semaphore_signal(barrier, inc=1, device_id=partner, device_id_type=LOGICAL)
+    for one in loads[:3]:
+        one.wait()
     make_right(x_ref, in_gain_ref, wr_ref, ready_ref, rows_ref, rmsg_ref)
     pl.semaphore_wait(barrier, 129)
 
@@ -229,13 +273,16 @@
         rin_ref[b, pl.ds(a * 9, 9)] = rmsg_ref[pl.ds(mine * 9, 9)]
 
     spread(
-        mine,
         0,
+        out_lines,
+        out_index,
+        out_device,
         lambda c: rmsg_ref.at[pl.ds(c * 9, 9)],
         rin_ref.at[b, pl.ds(a * 9, 9)],
-        lambda c: c * 2 + half,
         keep_right,
     )
+    for one in loads[3:]:
+        one.wait()
     make_left(wl_ref, ready_ref, rows_ref, lmsg_ref)
     slot = b * 8 + lax.rem(a, 8)
     for ih in range(3):
@@ -244,11 +291,12 @@
             lin_ref[ih, pl.ds(slot * 3, 3)] = lmsg_ref[ih, pl.ds(mine * 3, 3)]
 
         spread(
-            mine,
             1 + ih,
+            out_lines,
+            out_index,
+            out_device,
             lambda c: lmsg_ref.at[ih, pl.ds(c * 3, 3)],
             lin_ref.at[ih, pl.ds(slot * 3, 3)],
-            lambda c: c * 2 + half,
             keep_left,
         )
     make_gate(wg_ref, ready_ref, gate_ref)
@@ -267,11 +315,12 @@
             cin_ref[ih, pl.ds(mine * 3, 3)] = cmsg_ref[ih, pl.ds(home * 3, 3)]
 
         spread(
-            home,
             4 + ih,
+            back_lines,
+            back_index,
+            back_device,
             lambda c: cmsg_ref.at[ih, pl.ds(c * 3, 3)],
             cin_ref.at[ih, pl.ds(mine * 3, 3)],
-            lambda c: core * 128 + c,
             keep_product,
         )
     column = jnp.broadcast_to(mid_gain_ref[...], (128, 128)).T
@@ -287,10 +336,17 @@
     return pl.pallas_call(
         kernel,
         name="triangle",
-        out_shape=jax.ShapeDtypeStruct((48, 48, 128), BF16),
-        in_specs=[VMEM] * 7,
+        out_shape=pltpu.VMEM((48, 48, 128), BF16),
+        in_specs=[pl.BlockSpec(memory_space=pl.ANY)] * 7,
         out_specs=VMEM,
         scratch_shapes=[
+            pltpu.VMEM((48, 48, 128), BF16),
+            pltpu.VMEM((1, 128), F32),
+            pltpu.VMEM((128, 128), BF16),
+            pltpu.VMEM((128, 128), BF16),
+            pltpu.VMEM((1, 128), F32),
+            pltpu.VMEM((128, 128), BF16),
+            pltpu.VMEM((128, 128), BF16),
             pltpu.VMEM((18, 128, 128), BF16),
             pltpu.VMEM((48, 48, 128), F32),
             pltpu.VMEM((2304, 128), F32),
@@ -304,6 +360,7 @@
             pltpu.VMEM((8 * 136, 128), F32),
             pltpu.VMEM((3, 384, 2, 128), BF16),
             pltpu.VMEM((3, 384, 2, 128), BF16),
+            pltpu.SemaphoreType.DMA((7,)),
             pltpu.SemaphoreType.DMA((8,)),
             pltpu.SemaphoreType.DMA((8,)),
         ],

time: 60.9 us -> 60.7 us (level)
  local copies, waits for them, and re-layouts: 1.92 us -> 0.82 us
  Pallas kernels: 58.8 us -> 59.8 us
    unnamed x1, local copies, waits for them, and re-layouts: 1.92 us -> 0.82 us
    pallas_call x1, Pallas kernels: 58.8 us -> 59.8 us  [per_device(): pl.pallas_call(kernel, name='triangle', out_shape=pltpu.VMEM((48, 48, 128...]
where the time goes in v3:
time: 60.7 us
  Pallas kernels  59.8 us (99%)
  local copies, waits for them, and re-layouts  0.82 us (1%)
    pallas_call x1, Pallas kernels, per_device(): pl.pallas_call(kernel, name='triangle', out_shape=pltpu.VMEM((48, 48, 128...  59.8 us

profile of v3, /device:TPU:1, one launch (start us, length us, event | category | flops | bytes accessed | tf_op | source)
XLA Modules:
  0.0 60.7 jit_solution(6788494881940576568)
XLA Ops:
  0.0 59.8 %triangle.1 = bf16[48,48,128]{2,1,0:T(8,128)(2,1)S(1)} custom-call(bf16[48,48,128]{2,1,0:T(8,128)(2,1)} %x_hbm.1, f32[1,128]{1,0:T(1,128)} %bitcast.2, bf16[128,128]{1,0:T(8,128)(2,1)} %wl_hbm.1, bf16[128,128]{1,0:T(8,128)(2,1)} %wr_hbm.1, f32[1,128]{1,0:T(1,128)} %bitcast.3, bf16[128,128]{1,0:T(8,128)(2,1)} %wo_hbm.1, bf16[128,128]{1,0:T(8,128)(2,1)} %wg_hbm.1), custom_call_target="tpu_custom_call" | custom-call | tf_op jit(solution)/shard_map/triangle/pallas_call | solution.py:336
  59.8 0.8 %copy.9 = bf16[48,48,128]{2,1,0:T(8,128)(2,1)} copy(bf16[48,48,128]{2,1,0:T(8,128)(2,1)S(1)} %triangle.1) | data formatting | bytes 1179648

commit v4 on v3

--- a/solution.py
+++ b/solution.py
@@ -17,28 +17,33 @@
     return centred * scale * gain
 
 
-FAR_FIRST = [(dy, dx) for dy in (2, 1, 3, 0) for dx in (2, 1, 3, 0)]
-
-
 def ring(at, by, size):
     return jnp.where(at + by >= size, at + by - size, at + by)
 
 
-def outward(z, lines, step, last):
-    def plane(n, _):
-        m = (n + 1) // 2
-        there = ring(z, jnp.where(n % 2 == 0, 4 + m, 4 - m), 8)
-        for line in lines:
-            step(line, there)
-        return 0
-
-    lax.fori_loop(0, 7, plane, 0)
-    for line in lines[:-1]:
-        step(line, z)
-    last()
-
-
-def make_right(x_ref, gain_ref, w_ref, ready_ref, rows_ref, msg_ref):
+def inward(n):
+    return jnp.where(n == 0, 2, jnp.where(n == 1, 1, jnp.where(n == 2, 3, 0)))
+
+
+def heights(z):
+    return [ring(z, dz, 8) for dz in (4, 3, 5, 2, 6, 1, 7)] + [z]
+
+
+def outward(z, line_of, step, last):
+    there = heights(z)
+
+    def line(n, _):
+        for other in there:
+            step(line_of(n), other)
+        return 0
+
+    lax.fori_loop(0, 15, line, 0)
+    for other in there[:-1]:
+        step(line_of(jnp.int32(15)), other)
+    last(line_of(jnp.int32(15)), z)
+
+
+def make_right(x_ref, gain_ref, w_ref, ready_ref, rows_ref):
     gain = gain_ref[...]
     weights = w_ref[...].astype(F32).T.astype(BF16)
 
@@ -53,6 +58,8 @@
 
     lax.fori_loop(0, 3, tiles, 0)
 
+
+def pack_right(rows_ref, msg_ref):
     def pack(n, _):
         rows = rows_ref[pl.ds(pl.multiple_of(n * 288, 8), 288), :]
         msg_ref[pl.ds(n * 144, 144)] = rows.astype(BF16).reshape(144, 2, 128)
@@ -182,7 +189,7 @@
     x_hbm, in_gain_hbm, wl_hbm, wr_hbm, mid_gain_hbm, wo_hbm, wg_hbm, out_ref,
     x_ref, in_gain_ref, wl_ref, wr_ref, mid_gain_ref, wo_ref, wg_ref,
     ready_ref, gate_ref, rows_ref, rmsg_ref, lmsg_ref, rin_ref, lin_ref, pad_ref,
-    right_ref, left_ref, z_ref, cmsg_ref, cin_ref, load, send, recv,
+    right_ref, left_ref, z_ref, cmsg_ref, cin_ref, load, send, recv, ready_sem,
 ):
     hbm = (x_hbm, in_gain_hbm, wr_hbm, wl_hbm, mid_gain_hbm, wo_hbm, wg_hbm)
     vmem = (x_ref, in_gain_ref, wr_ref, wl_ref, mid_gain_ref, wo_ref, wg_ref)
@@ -197,22 +204,24 @@
     partner = a * 16 + b + 1 - 2 * core
     barrier = pltpu.get_barrier_semaphore()
 
-    out_lines = [ring(y, dy, 4) * 4 + ring(x, dx, 4) for dy, dx in FAR_FIRST]
-    near = lax.rem(y, 2)
-    back_lines = [
-        (ya * 4 + ring(x, dx, 4), c)
-        for ya in (1 - near, near)
-        for dx in (2, 1, 3, 0)
-        for c in (1 - core, core)
-    ]
-
-    def greet(line, there):
-        pl.semaphore_signal(
-            barrier,
-            inc=1,
-            device_id=core * 128 + line[0] * 16 + there * 2 + line[1],
-            device_id_type=LOGICAL,
-        )
+    def out_line(n):
+        return ring(y, inward(n // 4), 4) * 4 + ring(x, inward(n % 4), 4)
+
+    def back_line(n):
+        near = lax.rem(y, 2)
+        ya = jnp.where(n < 8, 1 - near, near)
+        c = jnp.where(n % 2 == 0, 1 - core, core)
+        return (ya * 4 + ring(x, inward((n // 2) % 4), 4)) * 16 + c
+
+    def greet(n, _):
+        for sem, device in ((barrier, a * 16 + ring(b, n, 16)), (barrier, ring(a, n, 16) * 16 + b)):
+            pl.semaphore_signal(sem, inc=1, device_id=device, device_id_type=LOGICAL)
+        return 0
+
+    def line_ready(n, _):
+        there = ring(a, n, 16) * 16 + b
+        pl.semaphore_signal(ready_sem.at[a], inc=1, device_id=there, device_id_type=LOGICAL)
+        return 0
 
     def copy(src, dst, n, device):
         return pltpu.make_async_remote_copy(
@@ -224,20 +233,20 @@
             device_id_type=LOGICAL,
         )
 
-    def spread(n, lines, index, device, src, dst, keep):
+    def spread(n, line_of, index, device, src, dst, keep):
         def step(line, there):
             copy(src(index(line, there)), dst, n, device(line, there)).start()
 
-        def last():
+        def last(line, there):
             @pl.when(jnp.logical_not(own))
             def _():
-                step(lines[-1], z)
+                step(line, there)
 
             @pl.when(own)
             def _():
                 keep()
 
-        outward(z, lines, step, last)
+        outward(z, line_of, step, last)
 
     def out_index(line, there):
         return line * 8 + there
@@ -246,7 +255,7 @@
         return line * 16 + there * 2 + half
 
     def back_index(line, there):
-        return line[0] * 16 + there * 2 + line[1]
+        return line + there * 2
 
     def back_device(line, there):
         return core * 128 + back_index(line, there)
@@ -262,25 +271,39 @@
             view = ref.at[pl.ds(0, 128 * rows)]
             pltpu.make_async_copy(view, view, sem).wait()
 
-    outward(z, back_lines, greet, lambda: greet(back_lines[-1], z))
-    pl.semaphore_signal(barrier, inc=1, device_id=partner, device_id_type=LOGICAL)
+    lax.fori_loop(1, 16, greet, 0)
     for one in loads[:3]:
         one.wait()
-    make_right(x_ref, in_gain_ref, wr_ref, ready_ref, rows_ref, rmsg_ref)
-    pl.semaphore_wait(barrier, 129)
-
-    def keep_right():
+    make_right(x_ref, in_gain_ref, wr_ref, ready_ref, rows_ref)
+    pl.semaphore_wait(barrier, 30)
+    lax.fori_loop(1, 16, line_ready, 0)
+    pack_right(rows_ref, rmsg_ref)
+
+    def send_right(line, there):
+        c = out_index(line, there)
+        dst = rin_ref.at[b, pl.ds(a * 9, 9)]
+        copy(rmsg_ref.at[pl.ds(c * 9, 9)], dst, 0, out_device(line, there)).start()
+
+    there = heights(z)
+    for other in there[:-1]:
+        send_right(a, other)
+
+    @pl.when(jnp.logical_not(own))
+    def _():
+        send_right(a, z)
+
+    @pl.when(own)
+    def _():
         rin_ref[b, pl.ds(a * 9, 9)] = rmsg_ref[pl.ds(mine * 9, 9)]
 
-    spread(
-        0,
-        out_lines,
-        out_index,
-        out_device,
-        lambda c: rmsg_ref.at[pl.ds(c * 9, 9)],
-        rin_ref.at[b, pl.ds(a * 9, 9)],
-        keep_right,
-    )
+    def right_line(n, _):
+        line = out_line(14 - n)
+        pl.semaphore_wait(ready_sem.at[line], 1)
+        for other in there:
+            send_right(line, other)
+        return 0
+
+    lax.fori_loop(0, 15, right_line, 0)
     for one in loads[3:]:
         one.wait()
     make_left(wl_ref, ready_ref, rows_ref, lmsg_ref)
@@ -292,7 +315,7 @@
 
         spread(
             1 + ih,
-            out_lines,
+            out_line,
             out_index,
             out_device,
             lambda c: lmsg_ref.at[ih, pl.ds(c * 3, 3)],
@@ -316,7 +339,7 @@
 
         spread(
             4 + ih,
-            back_lines,
+            back_line,
             back_index,
             back_device,
             lambda c: cmsg_ref.at[ih, pl.ds(c * 3, 3)],
@@ -363,6 +386,7 @@
             pltpu.SemaphoreType.DMA((7,)),
             pltpu.SemaphoreType.DMA((8,)),
             pltpu.SemaphoreType.DMA((8,)),
+            pltpu.SemaphoreType.REGULAR((16,)),
         ],
         compiler_params=pltpu.CompilerParams(collective_id=1, has_side_effects=True),
     )(

time: 60.7 us -> 55.4 us (0.913)
  Pallas kernels: 59.8 us -> 54.5 us
    pallas_call x1, Pallas kernels: 59.8 us -> 54.5 us  [per_device(): pl.pallas_call(kernel, name='triangle', out_shape=pltpu.VMEM((48, 48, 128...]
where the time goes in v4:
time: 55.4 us; the launch traced here: 55.3 us
  Pallas kernels  54.5 us (98%)
  local copies, waits for them, and re-layouts  0.82 us (1%)
    pallas_call x1, Pallas kernels, per_device(): pl.pallas_call(kernel, name='triangle', out_shape=pltpu.VMEM((48, 48, 128...  54.5 us

profile of v4, /device:TPU:1, one launch (start us, length us, event | category | flops | bytes accessed | tf_op | source)
XLA Modules:
  0.0 55.3 jit_solution(2881925960051261860)
XLA Ops:
  0.0 54.5 %triangle.1 = bf16[48,48,128]{2,1,0:T(8,128)(2,1)S(1)} custom-call(bf16[48,48,128]{2,1,0:T(8,128)(2,1)} %x_hbm.1, f32[1,128]{1,0:T(1,128)} %bitcast.2, bf16[128,128]{1,0:T(8,128)(2,1)} %wl_hbm.1, bf16[128,128]{1,0:T(8,128)(2,1)} %wr_hbm.1, f32[1,128]{1,0:T(1,128)} %bitcast.3, bf16[128,128]{1,0:T(8,128)(2,1)} %wo_hbm.1, bf16[128,128]{1,0:T(8,128)(2,1)} %wg_hbm.1), custom_call_target="tpu_custom_call" | custom-call | tf_op jit(solution)/shard_map/triangle/pallas_call | solution.py:359
  54.5 0.8 %copy.9 = bf16[48,48,128]{2,1,0:T(8,128)(2,1)} copy(bf16[48,48,128]{2,1,0:T(8,128)(2,1)S(1)} %triangle.1) | data formatting | bytes 1179648

commit v5 on v4

--- a/solution.py
+++ b/solution.py
@@ -43,11 +43,12 @@
     last(line_of(jnp.int32(15)), z)
 
 
-def make_right(x_ref, gain_ref, w_ref, ready_ref, rows_ref):
+def make_right(part, x_ref, gain_ref, w_ref, ready_ref, rows_ref):
     gain = gain_ref[...]
     weights = w_ref[...].astype(F32).T.astype(BF16)
 
     def tiles(k1, _):
+        part(k1).wait()
         for i1 in range(6):
             block = x_ref[i1 * 8 : i1 * 8 + 8, pl.ds(pl.multiple_of(k1 * 16, 16), 16), :]
             ready = norm(block.astype(F32).reshape(128, 128), gain, 1).astype(BF16)
@@ -59,13 +60,9 @@
     lax.fori_loop(0, 3, tiles, 0)
 
 
-def pack_right(rows_ref, msg_ref):
-    def pack(n, _):
-        rows = rows_ref[pl.ds(pl.multiple_of(n * 288, 8), 288), :]
-        msg_ref[pl.ds(n * 144, 144)] = rows.astype(BF16).reshape(144, 2, 128)
-        return 0
-
-    lax.fori_loop(0, 8, pack, 0)
+def pack_right(line, rows_ref, msg_ref):
+    rows = rows_ref[pl.ds(pl.multiple_of(line * 144, 8), 144), :]
+    msg_ref[pl.ds(line * 72, 72)] = rows.astype(BF16).reshape(72, 2, 128)
 
 
 def make_left(w_ref, ready_ref, rows_ref, msg_ref):
@@ -191,8 +188,14 @@
     ready_ref, gate_ref, rows_ref, rmsg_ref, lmsg_ref, rin_ref, lin_ref, pad_ref,
     right_ref, left_ref, z_ref, cmsg_ref, cin_ref, load, send, recv, ready_sem,
 ):
-    hbm = (x_hbm, in_gain_hbm, wr_hbm, wl_hbm, mid_gain_hbm, wo_hbm, wg_hbm)
-    vmem = (x_ref, in_gain_ref, wr_ref, wl_ref, mid_gain_ref, wo_ref, wg_ref)
+    def part(k1):
+        at = pl.ds(pl.multiple_of(k1 * 16, 16), 16)
+        return pltpu.make_async_copy(x_hbm.at[:, at, :], x_ref.at[:, at, :], load.at[6 + k1])
+
+    for k1 in range(3):
+        part(k1).start()
+    hbm = (in_gain_hbm, wr_hbm, wl_hbm, mid_gain_hbm, wo_hbm, wg_hbm)
+    vmem = (in_gain_ref, wr_ref, wl_ref, mid_gain_ref, wo_ref, wg_ref)
     loads = [pltpu.make_async_copy(s, d, load.at[n]) for n, (s, d) in enumerate(zip(hbm, vmem))]
     for one in loads:
         one.start()
@@ -272,12 +275,11 @@
             pltpu.make_async_copy(view, view, sem).wait()
 
     lax.fori_loop(1, 16, greet, 0)
-    for one in loads[:3]:
+    for one in loads[:2]:
         one.wait()
-    make_right(x_ref, in_gain_ref, wr_ref, ready_ref, rows_ref)
+    make_right(part, x_ref, in_gain_ref, wr_ref, ready_ref, rows_ref)
     pl.semaphore_wait(barrier, 30)
     lax.fori_loop(1, 16, line_ready, 0)
-    pack_right(rows_ref, rmsg_ref)
 
     def send_right(line, there):
         c = out_index(line, there)
@@ -285,6 +287,8 @@
         copy(rmsg_ref.at[pl.ds(c * 9, 9)], dst, 0, out_device(line, there)).start()
 
     there = heights(z)
+    pack_right(a, rows_ref, rmsg_ref)
+    pack_right(out_line(jnp.int32(14)), rows_ref, rmsg_ref)
     for other in there[:-1]:
         send_right(a, other)
 
@@ -297,14 +301,19 @@
         rin_ref[b, pl.ds(a * 9, 9)] = rmsg_ref[pl.ds(mine * 9, 9)]
 
     def right_line(n, _):
+        pack_right(out_line(13 - n), rows_ref, rmsg_ref)
         line = out_line(14 - n)
         pl.semaphore_wait(ready_sem.at[line], 1)
         for other in there:
             send_right(line, other)
         return 0
 
-    lax.fori_loop(0, 15, right_line, 0)
-    for one in loads[3:]:
+    lax.fori_loop(0, 14, right_line, 0)
+    line = out_line(jnp.int32(0))
+    pl.semaphore_wait(ready_sem.at[line], 1)
+    for other in there:
+        send_right(line, other)
+    for one in loads[2:]:
         one.wait()
     make_left(wl_ref, ready_ref, rows_ref, lmsg_ref)
     slot = b * 8 + lax.rem(a, 8)
@@ -383,7 +392,7 @@
             pltpu.VMEM((8 * 136, 128), F32),
             pltpu.VMEM((3, 384, 2, 128), BF16),
             pltpu.VMEM((3, 384, 2, 128), BF16),
-            pltpu.SemaphoreType.DMA((7,)),
+            pltpu.SemaphoreType.DMA((9,)),
             pltpu.SemaphoreType.DMA((8,)),
             pltpu.SemaphoreType.DMA((8,)),
             pltpu.SemaphoreType.REGULAR((16,)),

time: 55.4 us -> 55.3 us (level)
  no operation moved by 1% of the time
where the time goes in v5:
time: 55.3 us; the launch traced here: 55.2 us
  Pallas kernels  54.3 us (98%)
  local copies, waits for them, and re-layouts  0.82 us (1%)
    pallas_call x1, Pallas kernels, per_device(): pl.pallas_call(kernel, name='triangle', out_shape=pltpu.VMEM((48, 48, 128...  54.3 us

profile of v5, /device:TPU:1, one launch (start us, length us, event | category | flops | bytes accessed | tf_op | source)
XLA Modules:
  0.0 55.2 jit_solution(13843986236721060317)
XLA Ops:
  0.0 54.3 %triangle.1 = bf16[48,48,128]{2,1,0:T(8,128)(2,1)S(1)} custom-call(bf16[48,48,128]{2,1,0:T(8,128)(2,1)} %x_hbm.1, f32[1,128]{1,0:T(1,128)} %bitcast.2, bf16[128,128]{1,0:T(8,128)(2,1)} %wl_hbm.1, bf16[128,128]{1,0:T(8,128)(2,1)} %wr_hbm.1, f32[1,128]{1,0:T(1,128)} %bitcast.3, bf16[128,128]{1,0:T(8,128)(2,1)} %wo_hbm.1, bf16[128,128]{1,0:T(8,128)(2,1)} %wg_hbm.1), custom_call_target="tpu_custom_call" | custom-call | tf_op jit(solution)/shard_map/triangle/pallas_call | solution.py:368
  54.3 0.8 %copy.9 = bf16[48,48,128]{2,1,0:T(8,128)(2,1)} copy(bf16[48,48,128]{2,1,0:T(8,128)(2,1)S(1)} %triangle.1) | data formatting | bytes 1179648
